TPU v7x, 512 devices: a whole 4x8x8 slice. The times are simulated.
512 devices in a mesh: ops: 128 (over x, z_hi, y), grp: 4 (over z_lo, core).
Axes of the slice: x: 4, y: 8, z: 8 (z_hi: 4, z_lo: 2; z = z_hi * 2 + z_lo), core: 2. Of those that a mesh axis runs over, the one named last changes fastest.
Arguments:
- wave: bfloat16 [32, 512, 512], P(None, 'ops'), may hold values from -12 to 12
- diag_energy: float32 [32, 512, 512], P(None, 'ops'), may hold values from 0.5 to 2
- left_ops: bfloat16 [512, 512, 512], P(('ops', 'grp')), may hold values from -0.046875 to 0.046875
- right_ops: bfloat16 [512, 512, 512], P(('ops', 'grp')), may hold values from -0.25 to 0.25
- pair_sectors: int32 [512, 2], replicated, may hold values from 0 to 31, all different within a row
- sector_slot: int32 [32], replicated, may hold values from 0 to 31, each once
Outputs:
- residual: float32 [32, 512, 512], P(None, 'ops', 'grp')
- sigma_out: float32 [32, 512, 512], P(None, 'ops', 'grp')
Inputs may be any that keep to these rules, and one draw needn't show every extreme that they name: `pair_sectors`: each row names two different sectors; every sector is named by some row. `sector_slot`: each slot once.
All inputs are finite; a program needn't handle non-finite values.
Results may differ from a plain program's by a relative error of at most 0.0062.
Values may be sent and summed in bfloat16 or wider, within the bound.
No kernel may reach another device: no remote copies, remote signals or barrier semaphores. Data moves between devices by JAX's collectives and lax.ppermute only.
A program may use at most 64 MiB of HBM per device.

v0:
```python
import jax
import jax.numpy as jnp
from jax import lax
from jax.sharding import Mesh
from jax.sharding import PartitionSpec as P

OPS = ("ops_0", "ops_1", "ops_2")
OPS_GRP = ("ops_0", "ops_1", "ops_2", "grp")


def from_everyone(value, axis):
    devices = lax.axis_size(axis)
    return lax.all_to_all(
        jnp.broadcast_to(value[None], (devices, *value.shape)), axis, 0, 0, tiled=True
    )


def taken_together(value, axis):
    everything = from_everyone(value, axis)
    return jnp.sum(everything, axis=0)


def over_axes(value, axes):
    for axis in axes:
        value = lax.psum(value, axis)
    return value


def segment_total(received, targets, sectors):
    choose = (targets[None, :] == jnp.arange(sectors, dtype=jnp.int32)[:, None]).astype(jnp.float32)
    return jnp.dot(
        choose, received, precision=lax.Precision.HIGHEST, preferred_element_type=jnp.float32
    )


def apply_pairs(vector, left_ops, right_ops, wanted):
    ops_count = lax.axis_size(OPS)
    sectors, rows_here, block_width = vector.shape
    pair_dev = left_ops.shape[0]
    cell_count = rows_here * block_width
    outgoing = jnp.take(vector, wanted.reshape(-1), axis=0).reshape(
        ops_count, pair_dev * 2, rows_here, block_width
    )
    fetched = lax.all_to_all(outgoing, OPS, split_axis=0, concat_axis=2, tiled=True)
    inner_half = jnp.einsum(
        "pij,pjk->pik", left_ops, fetched[:, 0], preferred_element_type=jnp.float32
    ).astype(jnp.bfloat16)
    forward = jnp.einsum("pik,pkl->pil", inner_half, right_ops, preferred_element_type=jnp.float32)
    flipped = jnp.einsum(
        "pji,pjk->pik", left_ops, fetched[:, 1], preferred_element_type=jnp.float32
    ).astype(jnp.bfloat16)
    adjoint = jnp.einsum("pik,plk->pil", flipped, right_ops, preferred_element_type=jnp.float32)
    stacked = jnp.stack((adjoint, forward), axis=1).reshape(
        pair_dev, 2, ops_count, rows_here, block_width
    )
    arrived = lax.all_to_all(
        stacked.astype(jnp.bfloat16), OPS, split_axis=2, concat_axis=2, tiled=True
    ).astype(stacked.dtype)
    targets = jnp.transpose(wanted, (1, 2, 0)).reshape(-1)
    summed = segment_total(arrived.reshape(-1, cell_count), targets, sectors)
    return summed.reshape(sectors, rows_here, block_width)


def reduce_group(partial_value):
    return taken_together(partial_value, "grp")


def body(wave, diag_energy, left_ops, right_ops, pair_sectors, sector_slot):
    ops_count = lax.axis_size(OPS)
    grp_count = lax.axis_size("grp")
    pair_dev = left_ops.shape[0]
    block_width = wave.shape[2]
    stored = jnp.take(sector_slot, pair_sectors, axis=0).reshape(ops_count, grp_count, pair_dev, 2)
    wanted = lax.dynamic_index_in_dim(stored, lax.axis_index("grp"), 1, keepdims=False)
    column_share = block_width // grp_count
    column_start = lax.axis_index("grp") * column_share
    applied_sum = reduce_group(apply_pairs(wave, left_ops, right_ops, wanted))
    wave_wide = wave.astype(jnp.float32)
    applied = diag_energy * wave_wide + applied_sum
    products = (
        over_axes(jnp.sum(wave_wide * applied), OPS),
        over_axes(jnp.sum(wave_wide * wave_wide), OPS),
    )
    rayleigh = products[0] / products[1]
    residual = applied - rayleigh * wave_wide
    residual_half = residual.astype(jnp.bfloat16)
    second = reduce_group(apply_pairs(residual_half, left_ops, right_ops, wanted))
    sigma_out = diag_energy * residual_half.astype(jnp.float32) + second
    return (
        lax.dynamic_slice_in_dim(residual, column_start, column_share, 2),
        lax.dynamic_slice_in_dim(sigma_out, column_start, column_share, 2),
    )


def solution(mesh):
    finer = Mesh(
        mesh.devices.reshape(4, 4, 8, mesh.shape["grp"]), ("ops_0", "ops_1", "ops_2", "grp")
    )
    return jax.shard_map(
        body,
        mesh=finer,
        in_specs=(
            P(None, OPS, None),
            P(None, OPS, None),
            P(OPS_GRP, None, None),
            P(OPS_GRP, None, None),
            P(),
            P(),
        ),
        out_specs=(P(None, OPS, "grp"), P(None, OPS, "grp")),
        check_vma=False,
    )
```

profile of v0, /device:TPU:1, one launch (start us, length us, event | category | flops | bytes accessed | tf_op | source)
XLA Modules:
  0.0 287.8 jit_solution(8234370538445215668)
XLA Ops:
  0.7 0.7 copy-done.4
  1.4 0.7 fusion.45
  2.1 0.7 fusion.44
  3.5 20.1 %and_select_fusion = s32[512,2]{0,1:T(2,128)S(1)} fusion(s32[512,2]{0,1:T(2,128)S(1)} %copy-done.5, s32[]{:T(128)} %bitcast, s32[]{:T(128)} %bitcast.1, s32[]{:T(128)} %bitcast.2, s32[]{:T(128)} %bitcast.3, s32[]{:T(128)} %bitcast.4, s32[]{:T(128)} %bitcast.5, s32[]{:T(128)} %bitcast.6, s32[]{:T(128)} %bitcast.7, s32[]{:T(128)} %bitcast.8, s32[]{:T(128)} %bitcast.9, ...), kind=kLoop, calls=%fused_computation.90 | loop fusion | flops 70656 | bytes 8320 | tf_op jit(solution)/shard_map/jit(_take)/select_n | solution.py:73
  23.9 0.9 copy.73
  25.0 1.5 gather_fusion
  26.5 1.0 broadcast_select_fusion.1
  27.6 0.8 copy.74
  28.4 51.8 %all_to_all.56 = bf16[128,2,4,512]{3,1,2,0:T(2,128)(2,1)S(1)} all-to-all(bf16[128,2,4,512]{3,1,2,0:T(2,128)(2,1)S(1)} %copy.74), channel_id=1, replica_groups=mesh['ops_0'=4,'ops_1'=4,'ops_2'=8,'grp'=4] {'ops_0','ops_1','ops_2'}, dimensions={0} | all-to-all | bytes 2097152 | tf_op jit(solution)/shard_map/all_to_all | solution.py:44
  80.2 1.5 fusion.43
  82.9 0.9 copy-done.6
  84.9 0.8 copy.77
  85.7 37.7 %all_to_all.57 = bf16[1,2,128,4,512]{4,3,1,0,2:T(4,128)(2,1)S(1)} all-to-all(bf16[1,2,128,4,512]{4,3,1,0,2:T(4,128)(2,1)S(1)} %copy.77), channel_id=1, replica_groups=mesh['ops_0'=4,'ops_1'=4,'ops_2'=8,'grp'=4] {'ops_0','ops_1','ops_2'}, dimensions={2} | all-to-all | bytes 2097152 | tf_op jit(solution)/shard_map/all_to_all | solution.py:56
  125.1 19.2 %all_to_all.58 = f32[4,32,4,512]{3,1,2,0:T(8,128)S(1)} all-to-all(f32[4,32,4,512]{3,1,2,0:T(8,128)S(1)} %broadcast_in_dim.31), channel_id=1, replica_groups=mesh['ops_0'=4,'ops_1'=4,'ops_2'=8,'grp'=4] {'grp'}, dimensions={0} | all-to-all | bytes 2097152 | tf_op jit(solution)/shard_map/all_to_all | solution.py:13
  144.4 0.9 copy-done.2
  145.3 0.8 fusion.30
  146.1 7.0 %all-reduce.2 = (f32[]{:T(128)}, f32[]{:T(128)}) all-reduce(f32[]{:T(128)} %get-tuple-element.6, f32[]{:T(128)} %get-tuple-element.5), channel_id=1, replica_groups=mesh['ops_0'=4,'ops_1'=4,'ops_2'=8,'grp'=4] {'ops_0'}, use_global_device_ids=true, to_apply=%region_2.4 | all-reduce | flops 2 | bytes 16 | tf_op jit(solution)/shard_map/psum | solution.py:25
  153.1 9.5 %all-reduce.1 = (f32[]{:T(128)}, f32[]{:T(128)}) all-reduce(f32[]{:T(128)} %get-tuple-element.11, f32[]{:T(128)} %get-tuple-element.12), channel_id=1, replica_groups=mesh['ops_0'=4,'ops_1'=4,'ops_2'=8,'grp'=4] {'ops_1'}, use_global_device_ids=true, to_apply=%region_3.5 | all-reduce | flops 2 | bytes 16 | tf_op jit(solution)/shard_map/psum | solution.py:25
  162.5 11.6 %all-reduce = (f32[]{:T(128)}, f32[]{:T(128)}) all-reduce(f32[]{:T(128)} %get-tuple-element.9, f32[]{:T(128)} %get-tuple-element.10), channel_id=1, replica_groups=mesh['ops_0'=4,'ops_1'=4,'ops_2'=8,'grp'=4] {'ops_2'}, use_global_device_ids=true, to_apply=%region_4.6 | all-reduce | flops 2 | bytes 16 | tf_op jit(solution)/shard_map/psum | solution.py:25
  175.7 1.5 gather_fusion.1
  177.3 1.0 broadcast_select_fusion
  178.3 0.8 copy.81
  179.2 32.8 %all_to_all.59 = bf16[128,2,4,512]{3,1,2,0:T(2,128)(2,1)S(1)} all-to-all(bf16[128,2,4,512]{3,1,2,0:T(2,128)(2,1)S(1)} %copy.81), channel_id=1, replica_groups=mesh['ops_0'=4,'ops_1'=4,'ops_2'=8,'grp'=4] {'ops_0','ops_1','ops_2'}, dimensions={0} | all-to-all | bytes 2097152 | tf_op jit(solution)/shard_map/all_to_all | solution.py:44
  212.0 1.5 fusion.42
  213.5 1.3 fusion.3
  215.4 0.9 copy-done.7
  218.0 0.8 copy.84
  218.9 44.7 %all_to_all.60 = bf16[1,2,128,4,512]{4,3,1,0,2:T(4,128)(2,1)S(1)} all-to-all(bf16[1,2,128,4,512]{4,3,1,0,2:T(4,128)(2,1)S(1)} %copy.84), channel_id=1, replica_groups=mesh['ops_0'=4,'ops_1'=4,'ops_2'=8,'grp'=4] {'ops_0','ops_1','ops_2'}, dimensions={2} | all-to-all | bytes 2097152 | tf_op jit(solution)/shard_map/all_to_all | solution.py:56
  265.1 1.1 broadcast_in_dim.32
  266.2 7.2 %all-to-all-start.5 = ((f32[4,32,4,512]{3,1,2,0:T(8,128)}), f32[4,32,4,512]{3,1,2,0:T(8,128)S(1)}, u32[]{:S(2)}, u32[]{:S(2)}) async-start(f32[4,32,4,512]{3,1,2,0:T(8,128)} %broadcast_in_dim.32), calls=%async_computation.5 | async-start | bytes 2097152 | tf_op jit(solution)/shard_map/all_to_all | solution.py:13
  274.1 12.8 %all-to-all-done.5 = f32[4,32,4,512]{3,1,2,0:T(8,128)S(1)} async-done(((f32[4,32,4,512]{3,1,2,0:T(8,128)}), f32[4,32,4,512]{3,1,2,0:T(8,128)S(1)}, u32[]{:S(2)}, u32[]{:S(2)}) %all-to-all-start.5) | async-done | bytes 1048608 | tf_op jit(solution)/shard_map/all_to_all | solution.py:13
  287.1 0.7 copy_add_fusion
  (45 shorter events, 10.0 us)
Async XLA Ops:
  0.6 81.1 %copy-start = (bf16[1,512,512]{2,1,0:T(8,128)(2,1)S(1)}, bf16[1,512,512]{2,1,0:T(8,128)(2,1)}, u32[]{:S(2)}) copy-start(bf16[1,512,512]{2,1,0:T(8,128)(2,1)} %param.10) | copy-start | bytes 1572868
  0.6 0.7 copy-start.4
  2.8 0.7 copy-start.5
  23.9 1.1 copy-start.1
  82.8 1.0 copy-start.6
  144.3 1.0 copy-start.2
  215.2 1.0 copy-start.7
  216.3 1.0 copy-start.3
  266.2 20.7 %all-to-all-start.5 = ((f32[4,32,4,512]{3,1,2,0:T(8,128)}), f32[4,32,4,512]{3,1,2,0:T(8,128)S(1)}, u32[]{:S(2)}, u32[]{:S(2)}) async-start(f32[4,32,4,512]{3,1,2,0:T(8,128)} %broadcast_in_dim.32), calls=%async_computation.5 | async-start | bytes 2097152 | tf_op jit(solution)/shard_map/all_to_all | solution.py:13
where the time goes:
time: 289 us; the launch traced here: 288 us
  blocking collectives  214 us (74%)
  other arithmetic  24.4 us (8%)
  local copies, waits for them, and re-layouts  21.5 us (7%)
  waiting for transfers between devices  12.8 us (4%)
  starting transfers between devices  7.23 us (3%)
  matrix products  5.26 us (2%)
    all_to_all x2, blocking collectives, apply_pairs(): lax.all_to_all(outgoing, OPS, split_axis=0, concat_axis=2, tiled=True)  84.6 us
    all_to_all x2, blocking collectives, apply_pairs(): lax.all_to_all(stacked.astype(jnp.bfloat16), OPS, split_axis=2, concat_ax...  82.4 us
    psum x3, blocking collectives, over_axes(): value = lax.psum(value, axis)  28 us
    select_n x1, other arithmetic, body(): jnp.take(sector_slot, pair_sectors, axis=0)  20.1 us
    all_to_all x1, blocking collectives, from_everyone(): lax.all_to_all(jnp.broadcast_to(value[None], (devices, *value.shape)), ax...  19.2 us
    all_to_all x1, waiting for transfers between devices, from_everyone(): lax.all_to_all(jnp.broadcast_to(value[None], (devices, *value.shape)), ax...  12.8 us
    all_to_all x1, starting transfers between devices, from_everyone(): lax.all_to_all(jnp.broadcast_to(value[None], (devices, *value.shape)), ax...  7.23 us
  transfers between devices with their start and end apart: 1, of which 1 were waited for; matrix products, arithmetic and copies ran while one was open for 0% of the time, Pallas kernels for 0%

commit v1 on v0

--- a/solution.py
+++ b/solution.py
@@ -6,6 +6,12 @@
 
 OPS = ("ops_0", "ops_1", "ops_2")
 OPS_GRP = ("ops_0", "ops_1", "ops_2", "grp")
+
+
+def gather_and_add(value, mesh_axis):
+    parts = lax.all_gather(value, mesh_axis, axis=0, tiled=False)
+    acc = parts.sum(axis=0)
+    return acc
 
 
 def from_everyone(value, axis):
@@ -22,7 +28,7 @@
 
 def over_axes(value, axes):
     for axis in axes:
-        value = lax.psum(value, axis)
+        value = gather_and_add(value, axis)
     return value
 
 

time: 289 us -> 306 us (1.059)
  blocking collectives: 214 us -> 194 us
  local copies, waits for them, and re-layouts: 21.5 us -> 35.3 us
  waiting for transfers between devices: 12.8 us -> 24.1 us
  starting transfers between devices: 7.23 us -> 14 us
  other arithmetic: 24.4 us -> 29 us
    psum x3 -> x0, blocking collectives: 28 us -> none  [over_axes(): value = lax.psum(value, axis)]
    unnamed x0 -> x3, blocking collectives: none -> 26.1 us
    all_to_all x1 -> x0, blocking collectives: 19.2 us -> none  [from_everyone(): lax.all_to_all(jnp.broadcast_to(value[None], (devices, *value.shape)), ax...]
    all_to_all x1 -> x2, waiting for transfers between devices: 12.8 us -> 24.1 us  [from_everyone(): lax.all_to_all(jnp.broadcast_to(value[None], (devices, *value.shape)), ax...]
    unnamed x18 -> x33, local copies, waits for them, and re-layouts: 5.21 us -> 16.1 us
    all_to_all x1 -> x2, starting transfers between devices: 7.23 us -> 14 us  [from_everyone(): lax.all_to_all(jnp.broadcast_to(value[None], (devices, *value.shape)), ax...]
    reduce_sum x0 -> x6, other arithmetic: none -> 3.77 us  [gather_and_add(): acc = parts.sum(axis=0)]
  transfers between devices with their start and end apart: 1 -> 2, of which waited for: 1 -> 2; matrix products, arithmetic and copies ran while one was open for 0% -> 1% of each run, Pallas kernels for 0% -> 0%
where the time goes in v1:
time: 306 us; the launch traced here: 305 us
  blocking collectives  194 us (63%)
  local copies, waits for them, and re-layouts  35.3 us (12%)
  other arithmetic  29 us (9%)
  waiting for transfers between devices  24.1 us (8%)
  starting transfers between devices  14 us (5%)
  matrix products  6.29 us (2%)
    all_to_all x2, blocking collectives, apply_pairs(): lax.all_to_all(outgoing, OPS, split_axis=0, concat_axis=2, tiled=True)  84.5 us
    all_to_all x2, blocking collectives, apply_pairs(): lax.all_to_all(stacked.astype(jnp.bfloat16), OPS, split_axis=2, concat_ax...  83.1 us
    unnamed x3, blocking collectives  26.1 us
    all_to_all x2, waiting for transfers between devices, from_everyone(): lax.all_to_all(jnp.broadcast_to(value[None], (devices, *value.shape)), ax...  24.1 us
    select_n x1, other arithmetic, body(): jnp.take(sector_slot, pair_sectors, axis=0)  20.1 us
    unnamed x33, local copies, waits for them, and re-layouts  16.1 us
    all_to_all x2, starting transfers between devices, from_everyone(): lax.all_to_all(jnp.broadcast_to(value[None], (devices, *value.shape)), ax...  14 us
  transfers between devices with their start and end apart: 2, of which 2 were waited for; matrix products, arithmetic and copies ran while one was open for 1% of the time, Pallas kernels for 0%

profile of v1, /device:TPU:1, one launch (start us, length us, event | category | flops | bytes accessed | tf_op | source)
XLA Modules:
  0.0 304.7 jit_solution(7128570922926947598)
XLA Ops:
  0.7 1.8 fusion.45
  3.9 20.1 %and_select_fusion = s32[512,2]{0,1:T(2,128)S(1)} fusion(s32[512,2]{0,1:T(2,128)S(1)} %copy-done.5, s32[]{:T(128)} %bitcast, s32[]{:T(128)} %bitcast.1, s32[]{:T(128)} %bitcast.2, s32[]{:T(128)} %bitcast.3, s32[]{:T(128)} %bitcast.4, s32[]{:T(128)} %bitcast.5, s32[]{:T(128)} %bitcast.6, s32[]{:T(128)} %bitcast.7, s32[]{:T(128)} %bitcast.8, s32[]{:T(128)} %bitcast.9, ...), kind=kLoop, calls=%fused_computation.90 | loop fusion | flops 70656 | bytes 8320 | tf_op jit(solution)/shard_map/jit(_take)/select_n | solution.py:79
  25.5 1.5 gather_fusion
  27.0 1.0 broadcast_select_fusion.1
  28.9 51.8 %all_to_all.56 = bf16[128,2,4,512]{3,1,2,0:T(2,128)(2,1)S(1)} all-to-all(bf16[128,2,4,512]{3,1,2,0:T(2,128)(2,1)S(1)} %copy.74), channel_id=1, replica_groups=mesh['ops_0'=4,'ops_1'=4,'ops_2'=8,'grp'=4] {'ops_0','ops_1','ops_2'}, dimensions={0} | all-to-all | bytes 2097152 | tf_op jit(solution)/shard_map/all_to_all | solution.py:50
  80.7 1.5 fusion.43
  86.1 37.8 %all_to_all.57 = bf16[1,2,128,4,512]{4,3,1,0,2:T(4,128)(2,1)S(1)} all-to-all(bf16[1,2,128,4,512]{4,3,1,0,2:T(4,128)(2,1)S(1)} %copy.77), channel_id=1, replica_groups=mesh['ops_0'=4,'ops_1'=4,'ops_2'=8,'grp'=4] {'ops_0','ops_1','ops_2'}, dimensions={2} | all-to-all | bytes 2097152 | tf_op jit(solution)/shard_map/all_to_all | solution.py:62
  125.5 1.1 broadcast_in_dim.31
  126.6 6.8 %all-to-all-start.2 = ((f32[4,32,4,512]{3,1,2,0:T(8,128)}), f32[4,32,4,512]{3,1,2,0:T(8,128)S(1)}, u32[]{:S(2)}, u32[]{:S(2)}) async-start(f32[4,32,4,512]{3,1,2,0:T(8,128)} %broadcast_in_dim.31), calls=%async_computation.2 | async-start | bytes 2097152 | tf_op jit(solution)/shard_map/all_to_all | solution.py:19
  133.5 1.3 dynamic-slice
  134.8 12.1 %all-to-all-done.2 = f32[4,32,4,512]{3,1,2,0:T(8,128)S(1)} async-done(((f32[4,32,4,512]{3,1,2,0:T(8,128)}), f32[4,32,4,512]{3,1,2,0:T(8,128)S(1)}, u32[]{:S(2)}, u32[]{:S(2)}) %all-to-all-start.2) | async-done | bytes 1048608 | tf_op jit(solution)/shard_map/all_to_all | solution.py:19
  147.9 1.4 dynamic-update-slice
  149.4 1.4 dynamic-update-slice.3
  150.8 1.3 dynamic-slice.1
  152.1 6.3 %all-reduce.8 = (f32[4]{0:T(128)S(1)}, f32[4]{0:T(128)S(1)}) all-reduce(f32[4]{0:T(128)S(1)} %dynamic-update-slice, f32[4]{0:T(128)S(1)} %dynamic-update-slice.3), channel_id=1, replica_groups=mesh['ops_0'=4,'ops_1'=4,'ops_2'=8,'grp'=4] {'ops_0'}, use_global_device_ids=true, to_apply=%add | all-reduce | flops 8 | bytes 64
  159.7 1.4 dynamic-update-slice.1
  161.1 1.4 dynamic-update-slice.4
  162.5 1.3 dynamic-slice.2
  163.8 8.8 %all-reduce.7 = (f32[4]{0:T(128)S(1)}, f32[4]{0:T(128)S(1)}) all-reduce(f32[4]{0:T(128)S(1)} %dynamic-update-slice.1, f32[4]{0:T(128)S(1)} %dynamic-update-slice.4), channel_id=1, replica_groups=mesh['ops_0'=4,'ops_1'=4,'ops_2'=8,'grp'=4] {'ops_1'}, use_global_device_ids=true, to_apply=%add.1 | all-reduce | flops 8 | bytes 64
  173.9 1.4 dynamic-update-slice.2
  175.3 1.4 dynamic-update-slice.5
  176.8 11.0 %all-reduce.6 = (f32[8]{0:T(128)S(1)}, f32[8]{0:T(128)S(1)}) all-reduce(f32[8]{0:T(128)S(1)} %dynamic-update-slice.2, f32[8]{0:T(128)S(1)} %dynamic-update-slice.5), channel_id=1, replica_groups=mesh['ops_0'=4,'ops_1'=4,'ops_2'=8,'grp'=4] {'ops_2'}, use_global_device_ids=true, to_apply=%add.2 | all-reduce | flops 16 | bytes 128
  191.3 1.5 gather_fusion.1
  192.8 1.0 broadcast_select_fusion
  194.7 32.7 %all_to_all.58 = bf16[128,2,4,512]{3,1,2,0:T(2,128)(2,1)S(1)} all-to-all(bf16[128,2,4,512]{3,1,2,0:T(2,128)(2,1)S(1)} %copy.81), channel_id=1, replica_groups=mesh['ops_0'=4,'ops_1'=4,'ops_2'=8,'grp'=4] {'ops_0','ops_1','ops_2'}, dimensions={0} | all-to-all | bytes 2097152 | tf_op jit(solution)/shard_map/all_to_all | solution.py:50
  227.4 1.5 fusion.42
  229.5 2.3 fusion.5
  235.3 45.3 %all_to_all.59 = bf16[1,2,128,4,512]{4,3,1,0,2:T(4,128)(2,1)S(1)} all-to-all(bf16[1,2,128,4,512]{4,3,1,0,2:T(4,128)(2,1)S(1)} %copy.84), channel_id=1, replica_groups=mesh['ops_0'=4,'ops_1'=4,'ops_2'=8,'grp'=4] {'ops_0','ops_1','ops_2'}, dimensions={2} | all-to-all | bytes 2097152 | tf_op jit(solution)/shard_map/all_to_all | solution.py:62
  282.2 1.1 broadcast_in_dim.32
  283.3 7.1 %all-to-all-start.5 = ((f32[4,32,4,512]{3,1,2,0:T(8,128)}), f32[4,32,4,512]{3,1,2,0:T(8,128)S(1)}, u32[]{:S(2)}, u32[]{:S(2)}) async-start(f32[4,32,4,512]{3,1,2,0:T(8,128)} %broadcast_in_dim.32), calls=%async_computation.5 | async-start | bytes 2097152 | tf_op jit(solution)/shard_map/all_to_all | solution.py:19
  290.4 1.5 constant_dynamic-slice_fusion.1
  291.9 12.0 %all-to-all-done.5 = f32[4,32,4,512]{3,1,2,0:T(8,128)S(1)} async-done(((f32[4,32,4,512]{3,1,2,0:T(8,128)}), f32[4,32,4,512]{3,1,2,0:T(8,128)S(1)}, u32[]{:S(2)}, u32[]{:S(2)}) %all-to-all-start.5) | async-done | bytes 1048608 | tf_op jit(solution)/shard_map/all_to_all | solution.py:19
  (67 shorter events, 22.0 us)
Async XLA Ops:
  0.6 81.5 %copy-start = (bf16[1,512,512]{2,1,0:T(8,128)(2,1)S(1)}, bf16[1,512,512]{2,1,0:T(8,128)(2,1)}, u32[]{:S(2)}) copy-start(bf16[1,512,512]{2,1,0:T(8,128)(2,1)} %param.10) | copy-start | bytes 1572868
  0.6 1.9 copy-start.3
  3.3 0.7 copy-start.5
  24.4 1.1 copy-start.1
  83.2 1.0 copy-start.6
  126.6 20.3 %all-to-all-start.2 = ((f32[4,32,4,512]{3,1,2,0:T(8,128)}), f32[4,32,4,512]{3,1,2,0:T(8,128)S(1)}, u32[]{:S(2)}, u32[]{:S(2)}) async-start(f32[4,32,4,512]{3,1,2,0:T(8,128)} %broadcast_in_dim.31), calls=%async_computation.2 | async-start | bytes 2097152 | tf_op jit(solution)/shard_map/all_to_all | solution.py:19
  134.8 12.2 %copy-start.2 = (f32[32,4,512]{2,1,0:T(4,128)S(1)}, f32[32,4,512]{2,1,0:T(4,128)}, u32[]{:S(2)}) copy-start(f32[32,4,512]{2,1,0:T(4,128)} %param.9) | copy-start | bytes 786436
  232.2 1.0 copy-start.7
  233.3 1.0 copy-start.4
  283.3 20.6 %all-to-all-start.5 = ((f32[4,32,4,512]{3,1,2,0:T(8,128)}), f32[4,32,4,512]{3,1,2,0:T(8,128)S(1)}, u32[]{:S(2)}, u32[]{:S(2)}) async-start(f32[4,32,4,512]{3,1,2,0:T(8,128)} %broadcast_in_dim.32), calls=%async_computation.5 | async-start | bytes 2097152 | tf_op jit(solution)/shard_map/all_to_all | solution.py:19
